TPU v7x, 256 devices: a whole 4x4x8 slice. The times are simulated.
256 devices in a mesh: grp: 16 (over y, z_lo, core), sp: 16 (over z_hi, x).
Axes of the slice: x: 4, y: 4, z: 8 (z_hi: 4, z_lo: 2; z = z_hi * 2 + z_lo), core: 2. Of those that a mesh axis runs over, the one named last changes fastest.
Arguments:
- bucket_of: int32 [16], replicated, may hold values from 0 to 3, as said below
- lengths: int32 [4], replicated, may hold values from 256 to 1024, as said below
- counts: int32 [4], replicated, may hold values from 256 to 4096
- queries: bfloat16 [32768, 4096], P(('grp', 'sp')), may hold values from -4.5 to 4.5
- keys: bfloat16 [32768, 4096], P(('grp', 'sp')), may hold values from -4.5 to 4.5
- values: bfloat16 [32768, 4096], P(('grp', 'sp')), may hold values from -6 to 6
- out_grad: bfloat16 [32768, 3072], P(('grp', 'sp')), may hold values from -24 to 24
- w_out: bfloat16 [4096, 3072], P('sp', 'grp'), may hold values from -1.75 to 1.75
Outputs:
- grad_queries: bfloat16 [32768, 4096], P(('grp', 'sp'))
- grad_keys: bfloat16 [32768, 4096], P(('grp', 'sp'))
- grad_values: bfloat16 [32768, 4096], P(('grp', 'sp'))
- grad_w_out: float32 [4096, 3072], P('sp', 'grp')
Inputs may be any that keep to these rules, and one draw needn't show every extreme that they name: `bucket_of`: every one of the 4 buckets is held by at least one group. `lengths`: one bucket has length exactly 1024.
All inputs are finite; a program needn't handle non-finite values.
Results may differ from a plain program's by a relative error of at most 0.0091.
Values may be sent and summed in bfloat16 or wider, within the bound.
A program may use at most 128 MiB of HBM per device.

v0:
```python
import jax
import jax.numpy as jnp
from jax import lax
from jax.sharding import PartitionSpec as P

HEAD_DIM = 128
SEQS = 2


def copy_for_each(shard, axis):
    devices = lax.axis_size(axis)
    return lax.all_to_all(
        jnp.broadcast_to(shard[None], (devices, *shard.shape)), axis, 0, 0, tiled=True
    )


def joined_along(pieces, dim):
    lengths = list(pieces.shape[1:])
    lengths[dim] *= pieces.shape[0]
    return jnp.moveaxis(pieces, 0, dim).reshape(lengths)


def gather_directly(shard, axis, dim):
    pieces = copy_for_each(shard, axis)
    return joined_along(pieces, dim)


def dot_nt(first_op, second_op):
    return lax.dot_general(
        first_op, second_op, (((1,), (1,)), ((), ())), preferred_element_type=jnp.float32
    )


def dot_tn(first_op, second_op):
    return lax.dot_general(
        first_op, second_op, (((0,), (0,)), ((), ())), preferred_element_type=jnp.float32
    )


def probabilities(query_rows, key_rows, keep_cols):
    scores = dot_nt(query_rows, key_rows) * query_rows.shape[1] ** (-0.5)
    scores = jnp.where(keep_cols[None, :], scores, -jnp.inf)
    row_top = jnp.max(scores, axis=1, keepdims=True)
    row_exp = jnp.exp(scores - row_top)
    return row_exp / jnp.sum(row_exp, axis=1, keepdims=True)


def shards(bucket_of, lengths, counts, queries, keys, values, out_grad, w_out):
    group_index = lax.axis_index("grp")
    number_groups = lax.axis_size("grp")
    bucket_count = lengths.shape[0]
    bucket_table = (
        bucket_of[:, None] == jnp.arange(bucket_count, dtype=jnp.int32)[None, :]
    ).astype(jnp.int32)
    group_counts = jnp.sum(bucket_table * counts[None, :], axis=1)
    group_lengths = jnp.sum(bucket_table * lengths[None, :], axis=1)
    own_group = (jnp.arange(number_groups, dtype=jnp.int32) == group_index).astype(jnp.int32)
    seq_len = jnp.sum(own_group * group_lengths)
    weight = jnp.sum(own_group * group_counts).astype(jnp.float32) / jnp.sum(group_counts).astype(
        jnp.float32
    )
    heads_q, heads_k, heads_v = (
        lax.all_to_all(queries, "sp", split_axis=1, concat_axis=0, tiled=True),
        lax.all_to_all(keys, "sp", split_axis=1, concat_axis=0, tiled=True),
        lax.all_to_all(values, "sp", split_axis=1, concat_axis=0, tiled=True),
    )
    group_rows = heads_q.shape[0]
    width_local = heads_q.shape[1]
    capacity = group_rows // SEQS
    local_heads = width_local // HEAD_DIM
    item_count = SEQS * local_heads
    keep_cols = jnp.arange(capacity, dtype=jnp.int32) < seq_len
    keep_rows = jnp.tile(keep_cols, SEQS)
    row_scale = keep_rows[:, None].astype(jnp.float32)

    def item_corner(item_index):
        return (item_index // local_heads * capacity, item_index % local_heads * HEAD_DIM)

    def take_item(source, row_first, col_first):
        return lax.dynamic_slice(source, (row_first, col_first), (capacity, HEAD_DIM))

    def forward_item(item_index, attn_all):
        row_first, col_first = item_corner(item_index)
        query_rows = take_item(heads_q, row_first, col_first)
        key_rows = take_item(heads_k, row_first, col_first)
        value_rows = take_item(heads_v, row_first, col_first)
        probs_low = probabilities(query_rows, key_rows, keep_cols).astype(jnp.bfloat16)
        attn_item = jnp.dot(probs_low, value_rows, preferred_element_type=jnp.float32).astype(
            jnp.bfloat16
        )
        return lax.dynamic_update_slice(attn_all, attn_item, (row_first, col_first))

    attention = lax.fori_loop(
        0, item_count, forward_item, jnp.zeros((group_rows, width_local), jnp.bfloat16)
    )
    masked = attention * keep_rows[:, None].astype(jnp.bfloat16)
    w_rows = gather_directly(w_out, "grp", 1)
    gathered = lax.all_gather(out_grad, "sp", axis=0, tiled=True)
    d_full = dot_nt(gathered, w_rows)
    grad_local = dot_tn(masked, gathered)
    d_attn = (d_full * row_scale).astype(jnp.bfloat16)

    def backward_item(item_index, grad_heads):
        grad_q_all, grad_k_all, grad_v_all = grad_heads
        row_first, col_first = item_corner(item_index)
        query_rows = take_item(heads_q, row_first, col_first)
        key_rows = take_item(heads_k, row_first, col_first)
        value_rows = take_item(heads_v, row_first, col_first)
        attn_item = take_item(attention, row_first, col_first)
        d_item = take_item(d_attn, row_first, col_first)
        probs_full = probabilities(query_rows, key_rows, keep_cols)
        probs_low = probs_full.astype(jnp.bfloat16)
        row_delta = jnp.sum(
            d_item.astype(jnp.float32) * attn_item.astype(jnp.float32), axis=1, keepdims=True
        )
        dscore = (probs_full * (dot_nt(d_item, value_rows) - row_delta)).astype(jnp.bfloat16)
        factor = HEAD_DIM ** (-0.5)
        grad_q = (jnp.dot(dscore, key_rows, preferred_element_type=jnp.float32) * factor).astype(
            jnp.bfloat16
        )
        grad_k = (dot_tn(dscore, query_rows) * factor).astype(jnp.bfloat16)
        grad_v = dot_tn(probs_low, d_item).astype(jnp.bfloat16)
        grad_q_all = lax.dynamic_update_slice(grad_q_all, grad_q, (row_first, col_first))
        grad_k_all = lax.dynamic_update_slice(grad_k_all, grad_k, (row_first, col_first))
        grad_v_all = lax.dynamic_update_slice(grad_v_all, grad_v, (row_first, col_first))
        return (grad_q_all, grad_k_all, grad_v_all)

    empty_heads = jnp.zeros((group_rows, width_local), jnp.bfloat16)
    grad_q_all, grad_k_all, grad_v_all = lax.fori_loop(
        0, item_count, backward_item, (empty_heads, empty_heads, empty_heads)
    )
    back_q, back_k, back_v = (
        lax.all_to_all(grad_q_all, "sp", split_axis=0, concat_axis=1, tiled=True),
        lax.all_to_all(grad_k_all, "sp", split_axis=0, concat_axis=1, tiled=True),
        lax.all_to_all(grad_v_all, "sp", split_axis=0, concat_axis=1, tiled=True),
    )
    weighted = weight * grad_local
    grad_w = lax.psum_scatter(weighted, "grp", scatter_dimension=1, tiled=True)
    return (back_q, back_k, back_v, grad_w)


def solution(mesh):
    in_specs = (
        P(),
        P(),
        P(),
        P(("grp", "sp"), None),
        P(("grp", "sp"), None),
        P(("grp", "sp"), None),
        P(("grp", "sp"), None),
        P("sp", "grp"),
    )
    out_specs = (
        P(("grp", "sp"), None),
        P(("grp", "sp"), None),
        P(("grp", "sp"), None),
        P("sp", "grp"),
    )
    return jax.shard_map(shards, mesh=mesh, in_specs=in_specs, out_specs=out_specs, check_vma=False)
```

profile of v0, /device:TPU:8, one launch (start us, length us, event | category | flops | bytes accessed | tf_op | source)
XLA Modules:
  0.0 414.1 jit_solution(11999893446016128008)
XLA Ops:
  7.9 2.4 copy.64
  10.3 11.0 %all-to-all-start = ((bf16[128,16,256]{2,0,1:T(8,128)(2,1)}), bf16[128,16,256]{2,0,1:T(8,128)(2,1)S(1)}, u32[]{:S(2)}, u32[]{:S(2)}) async-start(bf16[128,16,256]{2,0,1:T(8,128)(2,1)} %bitcast.48), calls=%async_computation | async-start | bytes 2097152 | tf_op jit(solution)/shard_map/all_to_all | solution.py:63
  21.4 1.1 copy.63
  22.5 35.2 %all-to-all-done = bf16[128,16,256]{2,0,1:T(8,128)(2,1)S(1)} async-done(((bf16[128,16,256]{2,0,1:T(8,128)(2,1)}), bf16[128,16,256]{2,0,1:T(8,128)(2,1)S(1)}, u32[]{:S(2)}, u32[]{:S(2)}) %all-to-all-start) | async-done | bytes 1048608 | tf_op jit(solution)/shard_map/all_to_all | solution.py:63
  57.7 12.6 %all-to-all-start.1 = ((bf16[128,16,256]{2,0,1:T(8,128)(2,1)}), bf16[128,16,256]{2,0,1:T(8,128)(2,1)S(1)}, u32[]{:S(2)}, u32[]{:S(2)}) async-start(bf16[128,16,256]{2,0,1:T(8,128)(2,1)} %bitcast.47), calls=%async_computation.1 | async-start | bytes 2097152 | tf_op jit(solution)/shard_map/all_to_all | solution.py:64
  70.3 1.1 copy.62
  71.4 27.0 %all-to-all-done.1 = bf16[128,16,256]{2,0,1:T(8,128)(2,1)S(1)} async-done(((bf16[128,16,256]{2,0,1:T(8,128)(2,1)}), bf16[128,16,256]{2,0,1:T(8,128)(2,1)S(1)}, u32[]{:S(2)}, u32[]{:S(2)}) %all-to-all-start.1) | async-done | bytes 1048608 | tf_op jit(solution)/shard_map/all_to_all | solution.py:64
  98.4 6.2 %all-to-all-start.3 = ((bf16[128,16,256]{2,0,1:T(8,128)(2,1)}), bf16[128,16,256]{2,0,1:T(8,128)(2,1)S(1)}, u32[]{:S(2)}, u32[]{:S(2)}) async-start(bf16[128,16,256]{2,0,1:T(8,128)(2,1)} %bitcast.46), calls=%async_computation.3 | async-start | bytes 2097152 | tf_op jit(solution)/shard_map/all_to_all | solution.py:65
  108.6 45.1 %all-to-all-done.3 = bf16[128,16,256]{2,0,1:T(8,128)(2,1)S(1)} async-done(((bf16[128,16,256]{2,0,1:T(8,128)(2,1)}), bf16[128,16,256]{2,0,1:T(8,128)(2,1)S(1)}, u32[]{:S(2)}, u32[]{:S(2)}) %all-to-all-start.3) | async-done | bytes 1048608 | tf_op jit(solution)/shard_map/all_to_all | solution.py:65
  153.8 1.5 broadcast_in_dim.87
  155.2 7.9 %all-to-all-start.2 = ((bf16[16,256,192]{1,2,0:T(8,128)(2,1)}), bf16[16,256,192]{1,2,0:T(8,128)(2,1)}, u32[]{:S(2)}, u32[]{:S(2)}) async-start(bf16[16,256,192]{1,2,0:T(8,128)(2,1)} %broadcast_in_dim.87), calls=%async_computation.2 | async-start | bytes 3145728 | tf_op jit(solution)/shard_map/all_to_all | solution.py:12
  163.2 19.5 %while.36 = (s32[]{:T(128)}, bf16[2048,256]{1,0:T(8,128)(2,1)S(1)}, bf16[2048,256]{1,0:T(8,128)(2,1)S(1)}, bf16[2048,256]{1,0:T(8,128)(2,1)S(1)}, bf16[2048,256]...) while((s32[]{:T(128)}, bf16[2048,256]{1,0:T(8,128)(2,1)S(1)}, ...), condition=%wide.region_5.6_spmd.clone, body=%wide.region_2.5_spmd.clone.sunk | while | flops 549583872 | bytes 13660512 | solution.py:93
  163.9 0.7 fusion.69
  164.6 0.9 fusion.70
  165.5 2.5 fusion.71
  168.8 0.7 fusion.69
  169.5 0.9 fusion.70
  170.4 2.5 fusion.71
  173.6 0.7 fusion.69
  174.4 0.9 fusion.70
  175.3 2.5 fusion.71
  178.5 0.7 fusion.69
  179.2 0.9 fusion.70
  180.1 2.5 fusion.71
  182.7 56.8 %all-gather.2.cloned.1.call-done = bf16[2048,3072]{1,0:T(8,128)(2,1)} async-done(((bf16[128,3072]{1,0:T(8,128)(2,1)}), bf16[2048,3072]{1,0:T(8,128)(2,1)}) %all-gather.2.cloned.1.call-update) | async-done | bytes 12582928 | tf_op jit(solution)/shard_map/all_gather | solution.py:98
  239.5 11.6 %convolution_multiply_fusion.2 = f32[256,3072]{0,1:T(8,128)} fusion(bf16[2048,3072]{1,0:T(8,128)(2,1)} %all-gather.2.cloned.1.call-done, f32[]{:T(128)S(6)} %div.66, bf16[2048,256]{1,0:T(8,128)(2,1)S(1)} %get-tuple-element.655, bf16[2048]{0:T(1024)(128)(2,1)S(1)} %bitcast.67), kind=kOutput, calls=%fused_computation.43 | convolution fusion | flops 3222536192 | bytes 16781316 | tf_op jit(solution)/shard_map/dot_general | solution.py:35
  251.1 9.5 %fusion.39 = bf16[2048,256]{1,0:T(8,128)(2,1)} fusion(bf16[2048,3072]{1,0:T(8,128)(2,1)} %all-gather.2.cloned.1.call-done, bf16[256,3072]{0,1:T(8,128)(2,1)} %bitcast.5, f32[2048]{0:T(1024)S(1)} %bitcast.66), kind=kOutput, calls=%fused_computation.45 | convolution fusion | flops 3222274048 | bytes 15212544 | tf_op jit(solution)/shard_map/dot_general | solution.py:29
  260.5 1.0 broadcast.62.clone.1
  261.6 1.0 broadcast.62.clone
  262.6 1.0 broadcast.62
  263.7 42.5 %while.37 = (s32[]{:T(128)}, bf16[2048,256]{1,0:T(8,128)(2,1)}, bf16[2048,256]{1,0:T(8,128)(2,1)}, bf16[2048,256]{1,0:T(8,128)(2,1)}, bf16[2048,256]{1,0:T(8,128...) while((s32[]{:T(128)}, bf16[2048,256]{1,0:T(8,128)(2,1)}, ...), condition=%wide.region_10.11_spmd.clone, body=%wide.region_6.10_spmd.clone.sunk | while | flops 1363277824 | bytes 30461348 | solution.py:129
  264.3 1.2 multiply_reduce_fusion.2
  266.2 0.9 fusion.81
  267.1 1.9 fusion.84
  269.0 2.4 multiply_convert_fusion.2
  271.4 1.4 fusion.83
  272.8 1.5 fusion.82
  274.9 1.2 multiply_reduce_fusion.2
  276.1 0.7 fusion.80
  276.8 0.9 fusion.81
  277.8 1.9 fusion.84
  279.7 2.4 multiply_convert_fusion.2
  282.0 1.4 fusion.83
  283.4 1.5 fusion.82
  285.6 1.2 multiply_reduce_fusion.2
  287.5 0.9 fusion.81
  288.4 1.9 fusion.84
  290.3 2.4 multiply_convert_fusion.2
  292.6 1.4 fusion.83
  294.1 1.5 fusion.82
  296.2 1.2 multiply_reduce_fusion.2
  298.1 0.9 fusion.81
  299.0 1.9 fusion.84
  300.9 2.4 multiply_convert_fusion.2
  303.3 1.4 fusion.83
  304.7 1.5 fusion.82
  306.2 33.9 %all_to_all.119 = bf16[16,128,256]{2,1,0:T(8,128)(2,1)S(1)} all-to-all(bf16[16,128,256]{2,1,0:T(8,128)(2,1)} %bitcast.58), channel_id=1, replica_groups=mesh['grp'=16,'sp'=16] {'sp'}, dimensions={0} | all-to-all | bytes 2097152 | tf_op jit(solution)/shard_map/all_to_all | solution.py:133
  340.1 34.0 %all_to_all.120 = bf16[16,128,256]{2,1,0:T(8,128)(2,1)S(1)} all-to-all(bf16[16,128,256]{2,1,0:T(8,128)(2,1)} %bitcast.57), channel_id=1, replica_groups=mesh['grp'=16,'sp'=16] {'sp'}, dimensions={0} | all-to-all | bytes 2097152 | tf_op jit(solution)/shard_map/all_to_all | solution.py:135
  374.1 4.4 %all-to-all-start.5 = ((bf16[16,128,256]{2,1,0:T(8,128)(2,1)}), bf16[16,128,256]{2,1,0:T(8,128)(2,1)S(1)}, u32[]{:S(2)}, u32[]{:S(2)}) async-start(bf16[16,128,256]{2,1,0:T(8,128)(2,1)} %bitcast.14), calls=%async_computation.5 | async-start | bytes 2097152 | tf_op jit(solution)/shard_map/all_to_all | solution.py:134
  378.5 1.3 copy.45
  379.8 2.3 copy.48
  382.7 1.3 copy.50
  384.0 21.3 %all-to-all-done.5 = bf16[16,128,256]{2,1,0:T(8,128)(2,1)S(1)} async-done(((bf16[16,128,256]{2,1,0:T(8,128)(2,1)}), bf16[16,128,256]{2,1,0:T(8,128)(2,1)S(1)}, u32[]{:S(2)}, u32[]{:S(2)}) %all-to-all-start.5) | async-done | bytes 1048608 | tf_op jit(solution)/shard_map/all_to_all | solution.py:134
  405.9 1.3 copy.49
  (50 shorter events, 12.0 us)
Async XLA Ops:
  7.2 14.2 %copy-start.1 = (bf16[128,4096]{1,0:T(8,128)(2,1)S(1)}, bf16[128,4096]{1,0:T(8,128)(2,1)}, u32[]{:S(2)}) copy-start(bf16[128,4096]{1,0:T(8,128)(2,1)} %param.16) | copy-start | bytes 3145732
  7.2 232.3 %all-gather.2.cloned.1.call-start = ((), (), s32[]{:S(2)}) async-start(), calls=%async_computation.8 | async-start | bytes 13369344 | tf_op jit(solution)/shard_map/all_gather | solution.py:98
  7.9 62.4 %copy-start.2 = (bf16[128,4096]{1,0:T(8,128)(2,1)S(1)}, bf16[128,4096]{1,0:T(8,128)(2,1)}, u32[]{:S(2)}) copy-start(bf16[128,4096]{1,0:T(8,128)(2,1)} %param.17) | copy-start | bytes 3145732
  10.3 47.4 %all-to-all-start = ((bf16[128,16,256]{2,0,1:T(8,128)(2,1)}), bf16[128,16,256]{2,0,1:T(8,128)(2,1)S(1)}, u32[]{:S(2)}, u32[]{:S(2)}) async-start(bf16[128,16,256]{2,0,1:T(8,128)(2,1)} %bitcast.48), calls=%async_computation | async-start | bytes 2097152 | tf_op jit(solution)/shard_map/all_to_all | solution.py:63
  21.4 83.3 %copy-start.5 = (s32[4]{0:T(128)S(1)}, s32[4]{0:T(128)}, u32[]{:S(2)}) copy-start(s32[4]{0:T(128)} %param.14) | copy-start | bytes 52
  21.4 83.2 %copy-start.6 = (s32[16]{0:T(128)S(1)}, s32[16]{0:T(128)}, u32[]{:S(2)}) copy-start(s32[16]{0:T(128)} %param.12) | copy-start | bytes 196
  21.4 83.2 %copy-start.7 = (s32[4]{0:T(128)S(1)}, s32[4]{0:T(128)}, u32[]{:S(2)}) copy-start(s32[4]{0:T(128)} %param.13) | copy-start | bytes 52
  21.4 132.4 %copy-start.4 = (bf16[256,192]{0,1:T(8,128)(2,1)S(1)}, bf16[256,192]{0,1:T(8,128)(2,1)}, u32[]{:S(2)}) copy-start(bf16[256,192]{0,1:T(8,128)(2,1)} %param.19) | copy-start | bytes 294916
  57.7 40.7 %all-to-all-start.1 = ((bf16[128,16,256]{2,0,1:T(8,128)(2,1)}), bf16[128,16,256]{2,0,1:T(8,128)(2,1)S(1)}, u32[]{:S(2)}, u32[]{:S(2)}) async-start(bf16[128,16,256]{2,0,1:T(8,128)(2,1)} %bitcast.47), calls=%async_computation.1 | async-start | bytes 2097152 | tf_op jit(solution)/shard_map/all_to_all | solution.py:64
  98.4 55.3 %all-to-all-start.3 = ((bf16[128,16,256]{2,0,1:T(8,128)(2,1)}), bf16[128,16,256]{2,0,1:T(8,128)(2,1)S(1)}, u32[]{:S(2)}, u32[]{:S(2)}) async-start(bf16[128,16,256]{2,0,1:T(8,128)(2,1)} %bitcast.46), calls=%async_computation.3 | async-start | bytes 2097152 | tf_op jit(solution)/shard_map/all_to_all | solution.py:65
  153.8 9.4 %copy-start.3 = (bf16[128,16,256]{2,0,1:T(8,128)(2,1)}, bf16[128,16,256]{2,0,1:T(8,128)(2,1)S(1)}, u32[]{:S(2)}) copy-start(bf16[128,16,256]{2,0,1:T(8,128)(2,1)S(1)} %all-to-all-done.3) | copy-start | bytes 3145732
  155.2 95.8 %all-to-all-start.2 = ((bf16[16,256,192]{1,2,0:T(8,128)(2,1)}), bf16[16,256,192]{1,2,0:T(8,128)(2,1)}, u32[]{:S(2)}, u32[]{:S(2)}) async-start(bf16[16,256,192]{1,2,0:T(8,128)(2,1)} %broadcast_in_dim.87), calls=%async_computation.2 | async-start | bytes 3145728 | tf_op jit(solution)/shard_map/all_to_all | solution.py:12
  163.1 244.1 %reduce-scatter.2.cloned.1.call-start = ((), (), s32[]{:S(2)}) async-start(), calls=%async_computation.9 | async-start | bytes 3342336 | tf_op jit(solution)/shard_map/reduce_scatter | solution.py:138
  265.5 1.7 copy-start
  276.1 1.7 copy-start
  286.7 1.7 copy-start
  297.4 1.7 copy-start
  374.1 31.2 %all-to-all-start.5 = ((bf16[16,128,256]{2,1,0:T(8,128)(2,1)}), bf16[16,128,256]{2,1,0:T(8,128)(2,1)S(1)}, u32[]{:S(2)}, u32[]{:S(2)}) async-start(bf16[16,128,256]{2,1,0:T(8,128)(2,1)} %bitcast.14), calls=%async_computation.5 | async-start | bytes 2097152 | tf_op jit(solution)/shard_map/all_to_all | solution.py:134
Sparse Core Ops, SparseCore 0:
  10.4 229.0 all-gather.1
  251.2 61.2 reduce-scatter.1
where the time goes:
time: 415 us; the launch traced here: 414 us
  waiting for transfers between devices  186 us (45%)
  blocking collectives  67.9 us (16%)
  matrix products  65.6 us (16%)
  starting transfers between devices  42.1 us (10%)
  other arithmetic  19.5 us (5%)
  local copies, waits for them, and re-layouts  16.8 us (4%)
  between operations  15.6 us (4%)
    all_gather x1, waiting for transfers between devices, shards(): gathered = lax.all_gather(out_grad, 'sp', axis=0, tiled=True)  56.8 us
    all_to_all x1, waiting for transfers between devices, shards(): lax.all_to_all(values, 'sp', split_axis=1, concat_axis=0, tiled=True)  45.1 us
    all_to_all x1, waiting for transfers between devices, shards(): lax.all_to_all(queries, 'sp', split_axis=1, concat_axis=0, tiled=True)  35.2 us
    all_to_all x1, blocking collectives, shards(): lax.all_to_all(grad_v_all, 'sp', split_axis=0, concat_axis=1, tiled=True)  34 us
    all_to_all x1, blocking collectives, shards(): lax.all_to_all(grad_q_all, 'sp', split_axis=0, concat_axis=1, tiled=True)  33.9 us
    all_to_all x1, waiting for transfers between devices, shards(): lax.all_to_all(keys, 'sp', split_axis=1, concat_axis=0, tiled=True)  27 us
    dot_general x9, matrix products, dot_tn(): lax.dot_general(first_op, second_op, (((0,), (0,)), ((), ())), preferred_...  24.8 us
    dot_general x13, matrix products, dot_nt(): lax.dot_general(first_op, second_op, (((1,), (1,)), ((), ())), preferred_...  24.8 us
  transfers between devices with their start and end apart: 7, of which 5 were waited for; matrix products, arithmetic and copies ran while one was open for 25% of the time, Pallas kernels for 0%

commit v1 on v0

v1 whole, which is shorter than its diff:
```python
import jax
import jax.numpy as jnp
from jax import lax
from jax.experimental import pallas as pl
from jax.experimental.pallas import tpu as pltpu
from jax.sharding import PartitionSpec as P

MESH = pl.DeviceIdType.MESH
BF = jnp.bfloat16
F32 = jnp.float32
LOG2E = 1.4426950408889634
SCALE = 128 ** (-0.5)
NEG = -1e30
QT = 256


def dot_nn(a, b):
    return lax.dot_general(a, b, (((1,), (0,)), ((), ())), preferred_element_type=F32)


def dot_nt(a, b):
    return lax.dot_general(a, b, (((1,), (1,)), ((), ())), preferred_element_type=F32)


def kernel(
    bucket_ref, len_ref, cnt_ref, q_in, k_in, v_in, g_in, w_in,
    dq_out, dk_out, dv_out, gw_out,
    qb, kb, vb, kt, vt, gb, wb, do_t, pn, o_t, at_own, at_oth,
    w_own, w_got, bias, st_own, st_got, st_fin, ds,
    dq_own, dq_send, dq_got, dq_fin, dk_fin, dv_fin,
    gw_send, gw_got, gy_send, gy_got, gz, gz_got, fin_send, fin_got,
    s_loc, s_qkv, r_qkv, s_q2, r_q2, s_gz, r_gz, s_gx, r_gx, s_w, r_wc, r_wz, r_wy, r_wd,
    s_st, s_dq, r_dq, s_out, r_out, s_gc, r_gc, s_gy, r_gy, s_gzz, r_gzz, s_fin,
):
    g = lax.axis_index("grp")
    s = lax.axis_index("sp")
    core = lax.rem(g, 2)
    zl = lax.rem(lax.div(g, 2), 2)
    y = lax.div(g, 4)
    x = lax.rem(s, 4)
    zh = lax.div(s, 4)
    half = lax.rem(zh, 2)
    z = zh * 2 + zl

    def dev(x_=None, zh_=None, y_=None, zl_=None, core_=None):
        x_ = x if x_ is None else x_
        zh_ = zh if zh_ is None else zh_
        y_ = y if y_ is None else y_
        zl_ = zl if zl_ is None else zl_
        core_ = core if core_ is None else core_
        return {"grp": y_ * 4 + zl_ * 2 + core_, "sp": zh_ * 4 + x_}

    def zdev(z_):
        return dev(zh_=lax.div(z_, 2), zl_=lax.rem(z_, 2))

    def xs_of(d):
        return lax.rem(x + d, 4)

    def ys_of(d):
        return lax.rem(y + d, 4)

    def zs_of(d):
        return lax.rem(z + d, 8)

    other = dev(core_=1 - core)
    mate_zh = zh + 1 - 2 * half
    mate = dev(zh_=mate_zh)

    def m(v, k):
        return pl.multiple_of(v, k)

    sends = []

    def send(src, dst, ss, rs, device):
        c = pltpu.make_async_remote_copy(
            src_ref=src, dst_ref=dst, send_sem=ss, recv_sem=rs, device_id=device, device_id_type=MESH
        )
        c.start()
        return c

    def got(ref, sem):
        pltpu.make_async_copy(ref, ref, sem).wait()

    barrier = pltpu.get_barrier_semaphore()
    peers = [dev(x_=xs_of(d)) for d in (1, 2, 3)]
    peers += [dev(y_=ys_of(d)) for d in (1, 2, 3)]
    peers += [zdev(zs_of(d)) for d in range(1, 8)]
    peers += [other]
    for p in peers:
        pl.semaphore_signal(barrier, inc=1, device_id=p, device_id_type=MESH)
    pl.semaphore_wait(barrier, len(peers))

    seq_len = len_ref[bucket_ref[g]]
    total = cnt_ref[bucket_ref[0]]
    for i in range(1, 16):
        total = total + cnt_ref[bucket_ref[i]]
    weight = cnt_ref[bucket_ref[g]].astype(F32) / total.astype(F32)

    row_me = half * 512 + x * 128
    loc = []

    def local(src, dst, i):
        c = pltpu.make_async_copy(src, dst, s_loc.at[i])
        c.start()
        loc.append(c)
        return c

    for i in range(4):
        sends.append(send(
            g_in.at[pl.ds(i * 32, 32), :], gb.at[pl.ds(m(row_me + i * 32, 32), 32), :],
            s_gz.at[i], r_gz.at[i], mate))
    sends.append(send(
        w_in.at[pl.ds(m((1 - core) * 128, 128), 128), :], w_got, s_w.at[0], r_wc, other))
    lw = local(w_in.at[pl.ds(m(core * 128, 128), 128), :], w_own, 0)

    def blocks(src, dst, row, xp, a):
        out = []
        for b in range(4):
            out.append((src.at[:, pl.ds(m((b * 4 + xp) * 256, 256), 256)],
                        dst.at[pl.ds(row, 128), pl.ds(b * 256, 256)]))
        return out

    arrs = ((q_in, qb, m(row_me, 128)), (k_in, kb, m(x * 128, 128)), (v_in, vb, m(x * 128, 128)))

    def send_x(a):
        src, dst, row = arrs[a]
        for d in (1, 3, 2):
            xp = xs_of(d)
            for sr, dr in blocks(src, dst, row, xp, a):
                send(sr, dr, s_qkv.at[a * 4 + d], r_qkv.at[a, x], dev(x_=xp))

    for a in range(3):
        src, dst, row = arrs[a]
        for b, (sr, dr) in enumerate(blocks(src, dst, row, x, a)):
            local(sr, dr, 1 + a * 4 + b)
    lg = local(g_in, gb.at[pl.ds(m(row_me, 128), 128), :], 13)

    left, right = dev(x_=xs_of(3)), dev(x_=xs_of(1))

    def g_rows(hh, xs, i):
        return gb.at[pl.ds(m(hh * 512 + xs * 128 + i * 32, 32), 32), :]

    send_x(0)
    for i in range(4):
        for j, p in enumerate((right, left)):
            sends.append(send(
                g_in.at[pl.ds(i * 32, 32), :], g_rows(half, x, i),
                s_gx.at[i * 2 + j], r_gx.at[0, x, i], p))
    send_x(1)
    send_x(2)

    lw.wait()
    got(w_got, r_wc)
    r_i = lax.broadcasted_iota(jnp.int32, (192, 384), 0)
    c_i = lax.broadcasted_iota(jnp.int32, (192, 384), 1)
    e_own = jnp.where(c_i == r_i + core * 192, 1.0, 0.0).astype(BF)
    e_oth = jnp.where(c_i == r_i + (1 - core) * 192, 1.0, 0.0).astype(BF)

    def w_blk(zz):
        return wb.at[pl.ds(m(lax.div(zz, 2) * 256 + core * 128, 128), 128),
                     pl.ds(m((y * 2 + lax.rem(zz, 2)) * 384, 128), 384)]

    w_blk(z)[...] = (dot_nn(w_own[...], e_own) + dot_nn(w_got[...], e_oth)).astype(BF)
    for d in (4, 3, 5, 2, 6, 1, 7):
        sends.append(send(w_blk(z), w_blk(z), s_w.at[d], r_wz.at[z], zdev(zs_of(d))))

    for c in loc[1:5]:
        c.wait()

    def q_rows(hh, xs):
        return qb.at[pl.ds(m(hh * 512 + xs * 128, 128), 128), :]

    sends.append(send(q_rows(half, x), q_rows(half, x), s_q2.at[0], r_q2.at[x], mate))
    for d in (1, 3, 2):
        xs = xs_of(d)
        got(q_rows(half, xs), r_qkv.at[0, xs])
        sends.append(send(q_rows(half, xs), q_rows(half, xs), s_q2.at[d], r_q2.at[xs], mate))

    xr = xs_of(1)

    def w_row(ys, b):
        return wb.at[pl.ds(m(b * 256 + core * 128, 128), 128), pl.ds(m(ys * 768, 128), 768)]

    for i in range(4):
        got(g_rows(half, xr, i), r_gx.at[0, xr, i])
        sends.append(send(g_rows(half, xr, i), g_rows(half, xr, i), s_gx.at[8 + i], r_gx.at[0, xr, i], left))
        if i == 0:
            for d in range(1, 8):
                zz = zs_of(d)
                got(w_blk(zz), r_wz.at[zz])
            for b in range(4):
                for d in (2, 1, 3):
                    sends.append(send(w_row(y, b), w_row(y, b), s_w.at[8 + b * 4 + d], r_wy.at[y, b], dev(y_=ys_of(d))))
            for b in range(4):
                sends.append(send(w_row(y, b), w_row(y, b), s_w.at[8 + b * 4], r_wd.at[y, b], other))
        oh = 1 - half
        got(g_rows(oh, x, i), r_gz.at[i])
        for j, p in enumerate((right, left)):
            sends.append(send(g_rows(oh, x, i), g_rows(oh, x, i), s_gx.at[12 + i * 2 + j], r_gx.at[1, x, i], p))

    for c in loc[5:]:
        c.wait()
    for a, buf in ((1, kb), (2, vb)):
        for d in (1, 3, 2):
            xs = xs_of(d)
            got(buf.at[pl.ds(m(xs * 128, 128), 128), :], r_qkv.at[a, xs])

    key_pos = lax.broadcasted_iota(jnp.int32, (512, QT), 0) + half * 512
    bias[...] = jnp.where(key_pos < seq_len, 0.0, NEG)

    def col(h):
        return pl.ds(m(h * 128, 128), 128)

    def flip(h, c):
        kt[col(h), :] = kb[:, col(h)].T
        vt[col(h), :] = vb[:, col(h)].T
        return c

    lax.fori_loop(0, 8, flip, 0)

    def forward(q0):
        def body(h, c):
            sc = dot_nt(kb[:, col(h)], qb[pl.ds(q0, QT), col(h)])
            sc = sc * (SCALE * LOG2E) + bias[...]
            top = jnp.max(sc, axis=0, keepdims=True)
            pe = jnp.exp2(sc - top)
            st_own[pl.ds(h, 1), pl.ds(q0, QT)] = top
            st_own[pl.ds(8 + h, 1), pl.ds(q0, QT)] = jnp.sum(pe, axis=0, keepdims=True)
            pb = pe.astype(BF)
            pn[h, :, pl.ds(q0, QT)] = pb
            o_t[col(h), pl.ds(q0, QT)] = dot_nn(vt[col(h), :], pb)
            return c

        lax.fori_loop(0, 8, body, 0)

    own0 = m(half * 512, 256)
    oth0 = m((1 - half) * 512, 256)
    for t in range(2):
        forward(m(own0 + t * QT, 256))

    for d in (1, 3, 2):
        ys = ys_of(d)
        for b in range(4):
            got(w_row(ys, b), r_wy.at[ys, b])
            sends.append(send(w_row(ys, b), w_row(ys, b), s_w.at[24 + d * 4 + b], r_wd.at[ys, b], other))

    oh = 1 - half
    for i in range(4):
        got(g_rows(oh, xr, i), r_gx.at[1, xr, i])
        sends.append(send(g_rows(oh, xr, i), g_rows(oh, xr, i), s_gx.at[20 + i], r_gx.at[1, xr, i], left))

    def w_row_oth(ys, b):
        return wb.at[pl.ds(m(b * 256 + (1 - core) * 128, 128), 128), pl.ds(m(ys * 768, 128), 768)]

    for d in range(4):
        ys = ys_of(d)
        for b in range(4):
            got(w_row_oth(ys, b), r_wd.at[ys, b])

    for d in (2, 3):
        xs = xs_of(d)
        for i in range(4):
            got(g_rows(half, xs, i), r_gx.at[0, xs, i])

    def grads(q0):
        def body(i, c):
            rows = pl.ds(m(i * 256, 256), 256)
            do_t[rows, pl.ds(q0, 256)] = dot_nt(wb[rows, :], gb[pl.ds(q0, 256), :]).astype(BF)
            return c

        lax.fori_loop(0, 4, body, 0)

    for t in range(2):
        grads(m(own0 + t * 256, 256))

    for d in range(4):
        xs = xs_of(d)
        got(q_rows(oh, xs), r_q2.at[xs])
    for t in range(2):
        forward(m(oth0 + t * QT, 256))

    for d in (2, 3):
        xs = xs_of(d)
        for i in range(4):
            got(g_rows(oh, xs, i), r_gx.at[1, xs, i])
    for t in range(2):
        grads(m(oth0 + t * 256, 256))

    def delta(h, c):
        st_own[pl.ds(16 + h, 1), :] = jnp.sum(
            do_t[col(h), :].astype(F32) * o_t[col(h), :], axis=0, keepdims=True)
        return c

    lax.fori_loop(0, 8, delta, 0)
    sends.append(send(st_own, st_got, s_st.at[0], s_st.at[1], mate))
    got(st_got, s_st.at[1])

    top_own, top_got = st_own[pl.ds(0, 8), :], st_got[pl.ds(0, 8), :]
    top = jnp.maximum(top_own, top_got)
    a_own, a_got = jnp.exp2(top_own - top), jnp.exp2(top_got - top)
    length = st_own[pl.ds(8, 8), :] * a_own + st_got[pl.ds(8, 8), :] * a_got
    dsum = (st_own[pl.ds(16, 8), :] * a_own + st_got[pl.ds(16, 8), :] * a_got) / length
    q_pos = lax.rem(lax.broadcasted_iota(jnp.int32, (8, 1024), 1), 1024)
    fac = jnp.where(q_pos < seq_len, a_own / length, 0.0)
    st_fin[pl.ds(0, 8), :] = fac
    st_fin[pl.ds(8, 8), :] = dsum

    def masked(b, c):
        own = b * 2 + core
        oth = b * 2 + 1 - core
        rows = pl.ds(m(b * 128, 128), 128)
        at_own[rows, :] = (o_t[col(own), :] * st_fin[pl.ds(own, 1), :]).astype(BF)
        at_oth[rows, :] = (o_t[col(oth), :] * st_fin[pl.ds(oth, 1), :]).astype(BF)
        return c

    lax.fori_loop(0, 4, masked, 0)

    def weighted(at, r, ys):
        return dot_nn(at[pl.ds(m(r * 256, 256), 256), :], gb[:, pl.ds(m(ys * 768, 128), 768)]) * weight

    for d in (2, 1, 3, 0):
        ys = ys_of(d)

        def away(r, c):
            gw_send[d, pl.ds(m(r * 256, 256), 256), :] = weighted(at_oth, r, ys).astype(BF)
            return c

        lax.fori_loop(0, 2, away, 0)
        sends.append(send(gw_send.at[d], gw_got.at[d], s_gc.at[d], r_gc.at[d], other))

    def backward(h, c):
        for t in range(4):
            cols = pl.ds(t * QT, QT)
            dp = dot_nn(vb[:, col(h)], do_t[col(h), cols])
            f = st_fin[pl.ds(h, 1), cols]
            ds[:, cols] = (pn[h, :, cols].astype(F32) * f * (dp - st_fin[pl.ds(8 + h, 1), cols])).astype(BF)
        scaled = (do_t[col(h), :].astype(F32) * st_fin[pl.ds(h, 1), :]).astype(BF)
        dv_fin[:, col(h)] = dot_nt(pn[h], scaled).astype(BF)
        dk_fin[:, col(h)] = (dot_nn(ds[...], qb[:, col(h)]) * SCALE).astype(BF)
        mine = dot_nn(kt[col(h), :], ds[:, pl.ds(own0, 512)]) * SCALE
        away = dot_nn(kt[col(h), :], ds[:, pl.ds(oth0, 512)]) * SCALE
        dq_own[:, col(h)] = mine.T
        dq_send[:, col(h)] = away.T.astype(BF)
        return c

    outs = ((dq_fin, dq_out), (dk_fin, dk_out), (dv_fin, dv_out))

    def out_cols(b, xs):
        return pl.ds(m((b * 4 + xs) * 256, 256), 256)

    def give(a, b):
        src, dst = outs[a]
        for d in (1, 3, 2):
            xp = xs_of(d)
            sends.append(send(
                src.at[pl.ds(m(xp * 128, 128), 128), pl.ds(b * 256, 256)], dst.at[:, out_cols(b, x)],
                s_out.at[a, b, d], r_out.at[a, b, x], dev(x_=xp)))
        local(src.at[pl.ds(m(x * 128, 128), 128), pl.ds(b * 256, 256)], dst.at[:, out_cols(b, x)],
              14 + a * 4 + b)

    def finish(b):
        cols = pl.ds(b * 256, 256)
        got(dq_got.at[:, cols], r_dq.at[b])
        dq_fin[:, cols] = (dq_own[:, cols] + dq_got[:, cols].astype(F32)).astype(BF)
        give(0, b)

    def fold(d):
        ys = ys_of(d)
        got(gw_got.at[d], r_gc.at[d])

        def mine(r, c):
            rows = pl.ds(m(r * 256, 256), 256)
            gy_send[d, rows, :] = (weighted(at_own, r, ys) + gw_got[d, rows, :].astype(F32)).astype(BF)
            return c

        lax.fori_loop(0, 2, mine, 0)
        if d:
            sends.append(send(gy_send.at[d], gy_got.at[d], s_gy.at[d], r_gy.at[d], dev(y_=ys_of(d))))

    for b in range(4):
        lax.fori_loop(b * 2, b * 2 + 2, backward, 0)
        sends.append(send(
            dq_send.at[:, pl.ds(b * 256, 256)], dq_got.at[:, pl.ds(b * 256, 256)],
            s_dq.at[b], r_dq.at[b], mate))
        give(1, b)
        give(2, b)
        if b == 0:
            for d in (2, 1, 3, 0):
                fold(d)
        else:
            finish(b - 1)

    for d in (1, 3, 2):
        got(gy_got.at[d], r_gy.at[d])

    def gather_y(r, c):
        rows = pl.ds(m(r * 128, 128), 128)
        t = gy_send[0, rows, :].astype(F32)
        for d in (1, 2, 3):
            t = t + gy_got[d, rows, :].astype(F32)
        gz[rows, :] = t.astype(BF)
        return c

    lax.fori_loop(0, 4, gather_y, 0)

    def gz_blk(zz):
        return gz.at[pl.ds(m(lax.div(zz, 2) * 128, 128), 128), pl.ds(m(lax.rem(zz, 2) * 384, 128), 384)]

    for d in (4, 3, 5, 2, 6, 1, 7):
        zz = zs_of(d)
        sends.append(send(gz_blk(zz), gz_got.at[d], s_gzz.at[d], r_gzz.at[d], zdev(zz)))

    finish(3)

    for d in range(1, 8):
        got(gz_got.at[d], r_gzz.at[d])
    t = gz_blk(z)[...].astype(F32)
    for d in range(1, 8):
        t = t + gz_got[d].astype(F32)
    rolled = pltpu.roll(t, 192, 1)
    fin_send[...] = jnp.where(core == 0, rolled, t)[:, :192]
    sends.append(send(fin_send, fin_got, s_fin.at[0], s_fin.at[1], other))
    gw_out[pl.ds(m(core * 128, 128), 128), :] = jnp.where(core == 0, t, rolled)[:, :192]

    for b in range(4):
        for a in range(3):
            for d in (1, 3, 2):
                xs = xs_of(d)
                got(outs[a][1].at[:, out_cols(b, xs)], r_out.at[a, b, xs])
    got(fin_got, s_fin.at[1])
    gw_out[pl.ds(m((1 - core) * 128, 128), 128), :] = fin_got[...]

    for c in sends:
        c.wait_send()
    for a in range(3):
        for d in (1, 2, 3):
            got(q_rows(half, x), s_qkv.at[a * 4 + d])
    for c in loc[14:]:
        c.wait()


def shards(*args):
    any_ = pl.BlockSpec(memory_space=pl.ANY)
    smem = pl.BlockSpec(memory_space=pltpu.SMEM)
    tok = jax.ShapeDtypeStruct((128, 4096), BF)
    dma = pltpu.SemaphoreType.DMA
    return pl.pallas_call(
        kernel,
        out_shape=(tok, tok, tok, jax.ShapeDtypeStruct((256, 192), F32)),
        in_specs=[smem] * 3 + [any_] * 5,
        out_specs=(any_, any_, any_, pl.BlockSpec(memory_space=pltpu.VMEM)),
        scratch_shapes=[
            pltpu.VMEM((1024, 1024), BF), pltpu.VMEM((512, 1024), BF), pltpu.VMEM((512, 1024), BF),
            pltpu.VMEM((1024, 512), BF), pltpu.VMEM((1024, 512), BF),
            pltpu.VMEM((1024, 3072), BF), pltpu.VMEM((1024, 3072), BF),
            pltpu.VMEM((1024, 1024), BF), pltpu.VMEM((8, 512, 1024), BF), pltpu.VMEM((1024, 1024), F32),
            pltpu.VMEM((512, 1024), BF), pltpu.VMEM((512, 1024), BF),
            pltpu.VMEM((128, 192), BF), pltpu.VMEM((128, 192), BF), pltpu.VMEM((512, QT), F32),
            pltpu.VMEM((24, 1024), F32), pltpu.VMEM((24, 1024), F32), pltpu.VMEM((16, 1024), F32),
            pltpu.VMEM((512, 1024), BF),
            pltpu.VMEM((512, 1024), F32), pltpu.VMEM((512, 1024), BF), pltpu.VMEM((512, 1024), BF),
            pltpu.VMEM((512, 1024), BF), pltpu.VMEM((512, 1024), BF), pltpu.VMEM((512, 1024), BF),
            pltpu.VMEM((4, 512, 768), BF), pltpu.VMEM((4, 512, 768), BF),
            pltpu.VMEM((4, 512, 768), BF), pltpu.VMEM((4, 512, 768), BF),
            pltpu.VMEM((512, 768), BF), pltpu.VMEM((8, 128, 384), BF),
            pltpu.VMEM((128, 192), F32), pltpu.VMEM((128, 192), F32),
            dma((26,)), dma((12,)), dma((3, 4)), dma((4,)), dma((4,)), dma((4,)), dma((4,)),
            dma((24,)), dma((2, 4, 4)), dma((40,)), dma, dma((8,)), dma((4, 4)), dma((4, 4)),
            dma((2,)), dma((4,)), dma((4,)), dma((3, 4, 4)), dma((3, 4, 4)), dma((4,)), dma((4,)),
            dma((4,)), dma((4,)), dma((8,)), dma((8,)), dma((2,)),
        ],
        compiler_params=pltpu.CompilerParams(
            collective_id=0, has_side_effects=True, vmem_limit_bytes=67043328
        ),
    )(*args)


def solution(mesh):
    row = P(("grp", "sp"), None)
    return jax.shard_map(
        shards, mesh=mesh,
        in_specs=(P(), P(), P(), row, row, row, row, P("sp", "grp")),
        out_specs=(row, row, row, P("sp", "grp")),
        check_vma=False,
    )
```

time: 415 us -> 233 us (0.56)
  the two profiles are of different devices: /device:TPU:8 before, /device:TPU:1 now
where the time goes in v1:
time: 233 us
  Pallas kernels  224 us (96%)
  local copies, waits for them, and re-layouts  8.35 us (4%)
    pallas_call x1, Pallas kernels, shards(): pl.pallas_call(kernel, out_shape=(tok, tok, tok, jax.ShapeDtypeStruct((25...  224 us
    unnamed x8, local copies, waits for them, and re-layouts  6.6 us

profile of v1, /device:TPU:1, one launch (start us, length us, event | category | flops | bytes accessed | tf_op | source)
XLA Modules:
  0.0 232.5 jit_solution(15647703568695834813)
XLA Ops:
  0.6 1.7 copy.12.w_in
  2.3 223.5 %shard_map.111 = (bf16[128,4096]{1,0:T(8,128)(2,1)}, bf16[128,4096]{1,0:T(8,128)(2,1)}, bf16[128,4096]{1,0:T(8,128)(2,1)}, f32[256,192]{1,0:T(8,128)}) custom-call(s32[16]{0:T(128)} %bucket_ref.1, s32[4]{0:T(128)} %len_ref.1, s32[4]{0:T(128)} %cnt_ref.1, bf16[128,4096]{1,0:T(8,128)(2,1)} %q_in.1, bf16[128,4096]{1,0:T(8,128)(2,1)} %k_in.1, ...), custom_call_target="tpu_custom_call" | custom-call | tf_op jit(solution)/shard_map/pallas_call | solution.py:447
  225.8 1.7 copy.13
  227.6 0.0 copy-start.1
  227.6 2.4 %copy.17 = bf16[128,4096]{1,0:T(8,128)(2,1)} copy(bf16[128,4096]{1,0:T(8,128)(2,1)} %get-tuple-element.12) | data formatting | bytes 2097152
  230.0 0.0 copy-done.1
  230.0 0.0 copy-start
  230.0 1.0 copy.18
  230.9 0.6 copy-done
  231.6 1.0 copy.19
Async XLA Ops:
  227.6 2.4 %copy-start.1 = (bf16[128,4096]{1,0:T(8,128)(2,1)S(1)}, bf16[128,4096]{1,0:T(8,128)(2,1)}, u32[]{:S(2)}) copy-start(bf16[128,4096]{1,0:T(8,128)(2,1)} %get-tuple-element.13) | copy-start | bytes 3145732
  230.0 1.6 copy-start

commit v2 on v1

v2 whole, which is shorter than its diff:
```python
import jax
import jax.numpy as jnp
from jax import lax
from jax.experimental import pallas as pl
from jax.experimental.pallas import tpu as pltpu
from jax.sharding import PartitionSpec as P

MESH = pl.DeviceIdType.MESH
BF = jnp.bfloat16
F32 = jnp.float32
LOG2E = 1.4426950408889634
SCALE = 128 ** (-0.5)
NEG = -1e30
QT = 256


def dot_nn(a, b):
    return lax.dot_general(a, b, (((1,), (0,)), ((), ())), preferred_element_type=F32)


def dot_nt(a, b):
    return lax.dot_general(a, b, (((1,), (1,)), ((), ())), preferred_element_type=F32)


def dot_tn(a, b):
    return lax.dot_general(a, b, (((0,), (0,)), ((), ())), preferred_element_type=F32)


def kernel(
    bucket_ref, len_ref, cnt_ref, q_in, k_in, v_in, g_in, w_in,
    dq_out, dk_out, dv_out, gw_out,
    qb, kb, vb, kt, vt, gb, wb, do_t, pn, o_t, at,
    w_own, w_got, bias, st_own, st_got, st_fin, ds,
    dq_own, dq_send, dq_got, dq_fin, dk_fin, dv_fin,
    gw_send, gw_got, gy_send, gy_got, gz, gl_got, gz2, gz_got, fin, fin_got,
    s_loc, s_qkv, r_qkv, s_q2, r_q2, s_gz, r_gz, s_gx, r_gx, s_w, r_wc, r_wz, r_wl, r_wy, r_wd,
    s_st, r_st, s_dq, r_dq, s_out, r_out, s_gc, r_gc, s_gy, r_gy, s_gl, r_gl, s_g2, r_g2, s_fin,
):
    g = lax.axis_index("grp")
    s = lax.axis_index("sp")
    core = lax.rem(g, 2)
    zl = lax.rem(lax.div(g, 2), 2)
    y = lax.div(g, 4)
    x = lax.rem(s, 4)
    zh = lax.div(s, 4)
    half = lax.rem(zh, 2)
    pair = lax.div(zh, 2)

    def dev(x_=None, zh_=None, y_=None, zl_=None, core_=None):
        x_ = x if x_ is None else x_
        zh_ = zh if zh_ is None else zh_
        y_ = y if y_ is None else y_
        zl_ = zl if zl_ is None else zl_
        core_ = core if core_ is None else core_
        return {"grp": y_ * 4 + zl_ * 2 + core_, "sp": zh_ * 4 + x_}

    def xs_of(d):
        return lax.rem(x + d, 4)

    def ys_of(d):
        return lax.rem(y + d, 4)

    other = dev(core_=1 - core)
    mate_zh = zh + 1 - 2 * half
    mate = dev(zh_=mate_zh)
    zmate = dev(zl_=1 - zl)

    def m(v, k):
        return pl.multiple_of(v, k)

    sends = []

    def send(src, dst, ss, rs, device):
        c = pltpu.make_async_remote_copy(
            src_ref=src, dst_ref=dst, send_sem=ss, recv_sem=rs, device_id=device, device_id_type=MESH
        )
        c.start()
        return c

    def got(ref, sem):
        pltpu.make_async_copy(ref, ref, sem).wait()

    open_scope = []

    def mark(name):
        if open_scope:
            open_scope.pop().__exit__(None, None, None)
        if name:
            open_scope.append(jax.named_scope(name))
            open_scope[-1].__enter__()

    mark("barrier")
    barrier = pltpu.get_barrier_semaphore()
    peers = [dev(x_=xs_of(d)) for d in (1, 2, 3)]
    peers += [dev(y_=ys_of(d)) for d in (1, 2, 3)]
    peers += [dev(zh_=lax.rem(zh + d, 4)) for d in (1, 2, 3)]
    peers += [other, zmate]
    for p in peers:
        pl.semaphore_signal(barrier, inc=1, device_id=p, device_id_type=MESH)
    pl.semaphore_wait(barrier, len(peers))

    seq_len = len_ref[bucket_ref[g]]
    total = cnt_ref[bucket_ref[0]]
    for i in range(1, 16):
        total = total + cnt_ref[bucket_ref[i]]
    weight = cnt_ref[bucket_ref[g]].astype(F32) / total.astype(F32)

    row_me = half * 512 + x * 128
    loc = []

    def local(src, dst, i):
        c = pltpu.make_async_copy(src, dst, s_loc.at[i])
        c.start()
        loc.append(c)
        return c

    mark("first")

    def blocks(src, dst, row, xp):
        out = []
        for b in range(4):
            out.append((src.at[:, pl.ds(m((b * 4 + xp) * 256, 256), 256)],
                        dst.at[pl.ds(row, 128), pl.ds(b * 256, 256)]))
        return out

    arrs = ((q_in, qb, m(row_me, 128)), (k_in, kb, m(x * 128, 128)), (v_in, vb, m(x * 128, 128)))

    def send_x(a):
        src, dst, row = arrs[a]
        for d in (1, 3, 2):
            xp = xs_of(d)
            for sr, dr in blocks(src, dst, row, xp):
                send(sr, dr, s_qkv.at[a * 4 + d], r_qkv.at[a, x], dev(x_=xp))

    sends.append(send(
        w_in.at[:, pl.ds(m((1 - core) * 128, 128), 128)], w_got, s_w.at[0], r_wc, other))
    lw = local(w_in.at[:, pl.ds(m(core * 128, 128), 128)], w_own, 0)
    for a in range(3):
        send_x(a)
    for a in range(3):
        src, dst, row = arrs[a]
        for b, (sr, dr) in enumerate(blocks(src, dst, row, x)):
            local(sr, dr, 1 + a * 4 + b)
    local(g_in, gb.at[pl.ds(m(row_me, 128), 128), :], 13)

    mark("w_core")
    r_i = lax.broadcasted_iota(jnp.int32, (192, 384), 0)
    c_i = lax.broadcasted_iota(jnp.int32, (192, 384), 1)
    e_own = jnp.where(c_i == r_i + core * 192, 1.0, 0.0).astype(BF)
    e_oth = jnp.where(c_i == r_i + (1 - core) * 192, 1.0, 0.0).astype(BF)
    lw.wait()
    got(w_got, r_wc)

    def w_blk(zh_, zl_):
        return wb.at[pl.ds(m(zh_ * 256 + core * 128, 128), 128), pl.ds(m((y * 2 + zl_) * 384, 128), 384)]

    w_blk(zh, zl)[...] = (dot_tn(w_own[...], e_own) + dot_tn(w_got[...], e_oth)).astype(BF)
    for d in (2, 1, 3):
        sends.append(send(
            w_blk(zh, zl), w_blk(zh, zl), s_w.at[d], r_wz.at[zh], dev(zh_=lax.rem(zh + d, 4))))

    def g_mate(i):
        sends.append(send(
            g_in.at[pl.ds(i * 32, 32), :], gb.at[pl.ds(m(row_me + i * 32, 32), 32), :],
            s_gz.at[i], r_gz.at[i], mate))

    left, right = dev(x_=xs_of(3)), dev(x_=xs_of(1))
    xl, xr = xs_of(3), xs_of(1)
    oh = 1 - half

    def g_rows(hh, xs, i):
        return gb.at[pl.ds(m(hh * 512 + xs * 128 + i * 32, 32), 32), :]

    g_mate(0)
    for i in (0, 2, 1, 3):
        for j, p in enumerate((right, left)):
            sends.append(send(
                g_in.at[pl.ds(i * 32, 32), :], g_rows(half, x, i),
                s_gx.at[i * 2 + j], r_gx.at[0, x, i], p))
    mark("w_z_wait")
    for d in (1, 3, 2):
        zs = lax.rem(zh + d, 4)
        got(w_blk(zs, zl), r_wz.at[zs])
    for b in range(4):
        sends.append(send(w_blk(b, zl), w_blk(b, zl), s_w.at[4 + b], r_wl.at[b], zmate))
    for i in (1, 2, 3):
        g_mate(i)

    mark("w_l_wait")

    def w_row(ys, b):
        return wb.at[pl.ds(m(b * 256 + core * 128, 128), 128), pl.ds(m(ys * 768, 128), 768)]

    for b in range(4):
        got(w_blk(b, 1 - zl), r_wl.at[b])
        for d in (2, 1, 3):
            sends.append(send(
                w_row(y, b), w_row(y, b), s_w.at[8 + b * 4 + d], r_wy.at[y, b], dev(y_=ys_of(d))))
        sends.append(send(w_row(y, b), w_row(y, b), s_w.at[8 + b * 4], r_wd.at[y, b], other))

    mark("q_relay")
    for c in loc[1:5]:
        c.wait()

    def bt_of(t):
        return lax.rem(t + 2 * (1 - pair), 4)

    def q_rows(hh, xs):
        return qb.at[pl.ds(m(hh * 512 + xs * 128, 128), 128), :]

    for d in (1, 3, 2):
        got(q_rows(half, xs_of(d)), r_qkv.at[0, xs_of(d)])
    own0 = m(half * 512, 512)
    oth0 = m((1 - half) * 512, 512)

    def q_blk(r0, t):
        return qb.at[pl.ds(r0, 512), pl.ds(m(bt_of(t) * 256, 256), 256)]

    for t in range(4):
        sends.append(send(q_blk(own0, t), q_blk(own0, t), s_q2.at[t], r_q2.at[t], mate))

    def relay(hh, k, i, sem):
        src, to = (xr, left) if i < 2 else (xl, right)
        got(g_rows(hh, src, i), r_gx.at[k, src, i])
        sends.append(send(g_rows(hh, src, i), g_rows(hh, src, i), s_gx.at[sem + i], r_gx.at[k, src, i], to))

    mark("kv_wait")
    for c in loc[5:]:
        c.wait()
    n_loc = len(loc)
    for a, buf in ((1, kb), (2, vb)):
        for d in (1, 3, 2):
            xs = xs_of(d)
            got(buf.at[pl.ds(m(xs * 128, 128), 128), :], r_qkv.at[a, xs])

    mark("flip")
    key_pos = lax.broadcasted_iota(jnp.int32, (512, QT), 0) + half * 512
    bias[...] = jnp.where(key_pos < seq_len, 0.0, NEG)

    def col(h):
        return pl.ds(m(h * 128, 128), 128)

    def flip(h, c):
        kt[col(h), :] = kb[:, col(h)].T
        vt[col(h), :] = vb[:, col(h)].T
        return c

    lax.fori_loop(0, 8, flip, 0)

    def forward(t, first, r0):
        def body(n, c):
            j = lax.rem(n, 2)
            tt = t + lax.div(n, 4)
            h = bt_of(tt) * 2 + j
            q0 = m(r0 + lax.rem(lax.div(n, 2), 2) * QT, QT)
            sc = dot_nt(kb[:, col(h)], qb[pl.ds(q0, QT), col(h)])
            sc = sc * (SCALE * LOG2E) + bias[...]
            top = jnp.max(sc, axis=0, keepdims=True)
            pe = jnp.exp2(sc - top)
            st_own[tt, pl.ds(j, 1), pl.ds(q0, QT)] = top
            st_own[tt, pl.ds(2 + j, 1), pl.ds(q0, QT)] = jnp.sum(pe, axis=0, keepdims=True)
            pb = pe.astype(BF)
            pn[h, :, pl.ds(q0, QT)] = pb
            o_t[col(h), pl.ds(q0, QT)] = dot_nn(vt[col(h), :], pb)
            return c

        lax.fori_loop(0, first, body, 0)

    mark("fwd_own")
    forward(0, 16, own0)

    for i in (0, 1, 2, 3):
        mark(f"g_mate_{i}")
        got(g_rows(oh, x, i), r_gz.at[i])
        for j, p in enumerate((right, left)):
            sends.append(send(
                g_rows(oh, x, i), g_rows(oh, x, i), s_gx.at[12 + i * 2 + j], r_gx.at[1, x, i], p))
    for i in (0, 2, 1, 3):
        mark(f"g_relay_{i}")
        relay(half, 0, i, 8)

    mark("w_y_wait")
    for d in (1, 3, 2):
        ys = ys_of(d)
        for b in range(4):
            got(w_row(ys, b), r_wy.at[ys, b])
            sends.append(send(w_row(ys, b), w_row(ys, b), s_w.at[24 + d * 4 + b], r_wd.at[ys, b], other))

    def w_row_oth(ys, b):
        return wb.at[pl.ds(m(b * 256 + (1 - core) * 128, 128), 128), pl.ds(m(ys * 768, 128), 768)]

    def g_rest(hh, k):
        for i in range(4):
            got(g_rows(hh, xl if i < 2 else xr, i), r_gx.at[k, xl if i < 2 else xr, i])
            got(g_rows(hh, xs_of(2), i), r_gx.at[k, xs_of(2), i])

    def grads(q0):
        def body(i, c):
            rows = pl.ds(m(i * 256, 256), 256)
            do_t[rows, pl.ds(q0, 256)] = dot_nt(wb[rows, :], gb[pl.ds(q0, 256), :]).astype(BF)
            return c

        lax.fori_loop(0, 4, body, 0)

    mark("g_own_wait")
    g_rest(half, 0)
    for i in (0, 2):
        mark(f"g_relay2_{i}")
        relay(oh, 1, i, 20)
    mark("w_d2d_wait")
    for d in range(4):
        ys = ys_of(d)
        for b in range(4):
            got(w_row_oth(ys, b), r_wd.at[ys, b])
    mark("grads_own0")
    grads(own0)
    for i in (1, 3):
        mark(f"g_relay2_{i}")
        relay(oh, 1, i, 20)
    mark("grads_own1")
    grads(m(own0 + 256, 256))

    q_pos = lax.broadcasted_iota(jnp.int32, (2, 1024), 1)

    def weighted(ys):
        return dot_nn(at[...], gb[:, pl.ds(m(ys * 768, 128), 768)]) * weight

    outs = ((dq_fin, dq_out), (dk_fin, dk_out), (dv_fin, dv_out))

    def out_cols(b, xs):
        return pl.ds(m((b * 4 + xs) * 256, 256), 256)

    def give(a, t):
        b = bt_of(t)
        src, dst = outs[a]
        for d in (1, 3, 2):
            xp = xs_of(d)
            sends.append(send(
                src.at[pl.ds(m(xp * 128, 128), 128), pl.ds(m(b * 256, 256), 256)], dst.at[:, out_cols(b, x)],
                s_out.at[a, t, d], r_out.at[a, t, x], dev(x_=xp)))
        local(src.at[pl.ds(m(x * 128, 128), 128), pl.ds(m(b * 256, 256), 256)], dst.at[:, out_cols(b, x)],
              14 + a * 4 + t)

    def finish(t):
        mark(f"finish_{t}")
        cols = pl.ds(m(bt_of(t) * 256, 256), 256)
        got(dq_got.at[:, cols], r_dq.at[t])
        dq_fin[:, cols] = (dq_own[:, cols] + dq_got[:, cols].astype(F32)).astype(BF)
        give(0, t)

    def fold(t):
        mark(f"fold_{t}")
        got(gw_got.at[t], r_gc.at[t])
        for d in (2, 1, 3, 0):
            gy_send[t, d] = (gy_send[t, d].astype(F32) + gw_got[t, d].astype(F32)).astype(BF)
            if d:
                sends.append(send(
                    gy_send.at[t, d], gy_got.at[t, d], s_gy.at[t, d], r_gy.at[t, d], dev(y_=ys_of(d))))

    def gather_y(t):
        mark(f"gather_y_{t}")
        for d in (1, 3, 2):
            got(gy_got.at[t, d], r_gy.at[t, d])
        v = gy_send[t, 0].astype(F32)
        for d in (1, 2, 3):
            v = v + gy_got[t, d].astype(F32)
        gz[t, 0] = v[:, :384].astype(BF)
        gz[t, 1] = v[:, 384:].astype(BF)
        sends.append(send(gz.at[t, 1 - zl], gl_got.at[t], s_gl.at[t], r_gl.at[t], zmate))

    def fold_l(t):
        mark(f"fold_l_{t}")
        got(gl_got.at[t], r_gl.at[t])
        gz2[t] = (gz[t, zl].astype(F32) + gl_got[t].astype(F32)).astype(BF)
        if t < 2:
            sends.append(send(gz2.at[t], gz_got.at[half], s_g2.at[t], r_g2.at[half], dev(zh_=bt_of(t))))

    def query(t):
        mark(f"q_wait_{t}")
        got(q_blk(oth0, t), r_q2.at[t])
        mark(f"fwd_{t}")
        forward(t, 4, oth0)

    def stats(t):
        mark(f"grads_oth_{t}")
        bt = bt_of(t)
        rows = pl.ds(m(bt * 256, 256), 256)
        for u in range(2):
            q0 = m(oth0 + u * 256, 256)
            do_t[rows, pl.ds(q0, 256)] = dot_nt(wb[rows, :], gb[pl.ds(q0, 256), :]).astype(BF)
        for j in range(2):
            h = bt * 2 + j
            st_own[t, pl.ds(4 + j, 1), :] = jnp.sum(
                do_t[col(h), :].astype(F32) * o_t[col(h), :], axis=0, keepdims=True)
        sends.append(send(st_own.at[t], st_got.at[t], s_st.at[t], r_st.at[t], mate))

    def merge(t):
        mark(f"st_wait_{t}")
        got(st_got.at[t], r_st.at[t])
        top_own, top_got = st_own[t, 0:2, :], st_got[t, 0:2, :]
        top = jnp.maximum(top_own, top_got)
        a_own, a_got = jnp.exp2(top_own - top), jnp.exp2(top_got - top)
        length = st_own[t, 2:4, :] * a_own + st_got[t, 2:4, :] * a_got
        st_fin[t, 2:4, :] = (st_own[t, 4:6, :] * a_own + st_got[t, 4:6, :] * a_got) / length
        st_fin[t, 0:2, :] = jnp.where(q_pos < seq_len, a_own / length, 0.0)

    def back(t):
        mark(f"back_{t}")
        bt = bt_of(t)
        cols = pl.ds(m(bt * 256, 256), 256)

        def backward(j, c):
            h = bt * 2 + j
            for u in range(4):
                cu = pl.ds(u * QT, QT)
                dp = dot_nn(vb[:, col(h)], do_t[col(h), cu])
                f = st_fin[t, pl.ds(j, 1), cu]
                ds[:, cu] = (pn[h, :, cu].astype(F32) * f * (dp - st_fin[t, pl.ds(2 + j, 1), cu])).astype(BF)
            scaled = (do_t[col(h), :].astype(F32) * st_fin[t, pl.ds(j, 1), :]).astype(BF)
            away = dot_nn(kt[col(h), :], ds[:, pl.ds(oth0, 512)]) * SCALE
            dq_send[:, col(h)] = away.T.astype(BF)
            mine = dot_nn(kt[col(h), :], ds[:, pl.ds(own0, 512)]) * SCALE
            dq_own[:, col(h)] = mine.T
            dv_fin[:, col(h)] = dot_nt(pn[h], scaled).astype(BF)
            dk_fin[:, col(h)] = (dot_nn(ds[...], qb[:, col(h)]) * SCALE).astype(BF)
            return c

        lax.fori_loop(0, 2, backward, 0)
        sends.append(send(dq_send.at[:, cols], dq_got.at[:, cols], s_dq.at[t], r_dq.at[t], mate))
        give(1, t)
        give(2, t)

    def gw(t):
        mark(f"gw_{t}")
        bt = bt_of(t)
        at[0:128, :] = (o_t[col(bt * 2 + core), :] * st_fin[t, pl.ds(core, 1), :]).astype(BF)
        at[128:256, :] = (o_t[col(bt * 2 + 1 - core), :] * st_fin[t, pl.ds(1 - core, 1), :]).astype(BF)

        def gw_part(d, c):
            r = weighted(lax.rem(y + d, 4))
            gy_send[t, d] = r[:128].astype(BF)
            gw_send[t, d] = r[128:].astype(BF)
            return c

        lax.fori_loop(0, 4, gw_part, 0)
        sends.append(send(gw_send.at[t], gw_got.at[t], s_gc.at[t], r_gc.at[t], other))

    query(0)
    query(1)
    mark("g_oth_wait")
    g_rest(oh, 1)
    stats(0)
    stats(1)
    merge(0)
    back(0)
    gw(0)
    query(2)
    stats(2)
    merge(1)
    back(1)
    fold(0)
    gw(1)
    query(3)
    stats(3)
    merge(2)
    gw(2)
    back(2)
    fold(1)
    gather_y(0)
    finish(0)
    merge(3)
    gw(3)
    fold(2)
    back(3)
    gather_y(1)
    fold_l(0)
    fold(3)
    finish(1)
    gather_y(2)
    fold_l(1)
    gather_y(3)
    fold_l(2)
    finish(2)
    fold_l(3)
    sends.append(send(gz2.at[3 - half], gz_got.at[2], s_g2.at[2], r_g2.at[2], mate))
    finish(3)

    mark("gz_wait")
    for d in range(3):
        got(gz_got.at[d], r_g2.at[d])
    mark("gz_sum")
    v = gz2[2 + half].astype(F32)
    for d in range(3):
        v = v + gz_got[d].astype(F32)
    fin[...] = v.T
    sends.append(send(
        fin.at[pl.ds(m((1 - core) * 192, 64), 192), :], fin_got, s_fin.at[0], s_fin.at[1], other))
    gw_out[:, pl.ds(m(core * 128, 128), 128)] = fin[pl.ds(m(core * 192, 64), 192), :]

    mark("out_wait")
    for t in range(4):
        for a in (1, 2, 0):
            for d in (1, 3, 2):
                xs = xs_of(d)
                got(outs[a][1].at[:, out_cols(bt_of(t), xs)], r_out.at[a, t, xs])
    mark("fin_wait")
    got(fin_got, s_fin.at[1])
    gw_out[:, pl.ds(m((1 - core) * 128, 128), 128)] = fin_got[...]

    mark("send_wait")
    for c in sends:
        c.wait_send()
    for a in range(3):
        for d in (1, 2, 3):
            got(q_rows(half, x), s_qkv.at[a * 4 + d])
    for c in loc[n_loc:]:
        c.wait()
    mark(None)


def shards(*args):
    any_ = pl.BlockSpec(memory_space=pl.ANY)
    smem = pl.BlockSpec(memory_space=pltpu.SMEM)
    tok = jax.ShapeDtypeStruct((128, 4096), BF)
    dma = pltpu.SemaphoreType.DMA
    vm = pltpu.VMEM
    dq, dk, dv, gw = pl.pallas_call(
        kernel,
        out_shape=(tok, tok, tok, jax.ShapeDtypeStruct((192, 256), F32)),
        in_specs=[smem] * 3 + [any_] * 5,
        out_specs=(any_, any_, any_, pl.BlockSpec(memory_space=pltpu.VMEM)),
        scratch_shapes=[
            vm((1024, 1024), BF), vm((512, 1024), BF), vm((512, 1024), BF),
            vm((1024, 512), BF), vm((1024, 512), BF),
            vm((1024, 3072), BF), vm((1024, 3072), BF),
            vm((1024, 1024), BF), vm((8, 512, 1024), BF), vm((1024, 1024), F32),
            vm((256, 1024), BF),
            vm((192, 128), BF), vm((192, 128), BF), vm((512, QT), F32),
            vm((4, 8, 1024), F32), vm((4, 8, 1024), F32), vm((4, 8, 1024), F32),
            vm((512, 1024), BF),
            vm((512, 1024), F32), vm((512, 1024), BF), vm((512, 1024), BF),
            vm((512, 1024), BF), vm((512, 1024), BF), vm((512, 1024), BF),
            vm((4, 4, 128, 768), BF), vm((4, 4, 128, 768), BF),
            vm((4, 4, 128, 768), BF), vm((4, 4, 128, 768), BF),
            vm((4, 2, 128, 384), BF), vm((4, 128, 384), BF), vm((4, 128, 384), BF), vm((3, 128, 384), BF),
            vm((384, 128), F32), vm((192, 128), F32),
            dma((26,)), dma((12,)), dma((3, 4)), dma((4,)), dma((4,)), dma((4,)), dma((4,)),
            dma((24,)), dma((2, 4, 4)), dma((40,)), dma, dma((4,)), dma((4,)), dma((4, 4)), dma((4, 4)),
            dma((4,)), dma((4,)), dma((4,)), dma((4,)), dma((3, 4, 4)), dma((3, 4, 4)),
            dma((4,)), dma((4,)), dma((4, 4)), dma((4, 4)), dma((4,)), dma((4,)), dma((3,)), dma((3,)), dma((2,)),
        ],
        compiler_params=pltpu.CompilerParams(
            collective_id=0, has_side_effects=True, vmem_limit_bytes=67043328
        ),
    )(*args[:7], args[7].T)
    return dq, dk, dv, gw.T


def solution(mesh):
    row = P(("grp", "sp"), None)
    return jax.shard_map(
        shards, mesh=mesh,
        in_specs=(P(), P(), P(), row, row, row, row, P("sp", "grp")),
        out_specs=(row, row, row, P("sp", "grp")),
        check_vma=False,
    )
```

time: 233 us -> 186 us (0.80)
  Pallas kernels: 224 us -> 180 us
  local copies, waits for them, and re-layouts: 8.35 us -> 5.77 us
    pallas_call x1, Pallas kernels: 224 us -> 180 us  [shards(): pl.pallas_call(kernel, out_shape=(tok, tok, tok, jax.ShapeDtypeStruct((19...]
    unnamed x8 -> x10, local copies, waits for them, and re-layouts: 6.6 us -> 5.77 us
where the time goes in v2:
time: 186 us
  Pallas kernels  180 us (97%)
  local copies, waits for them, and re-layouts  5.77 us (3%)
    pallas_call x1, Pallas kernels, shards(): pl.pallas_call(kernel, out_shape=(tok, tok, tok, jax.ShapeDtypeStruct((19...  180 us
    unnamed x10, local copies, waits for them, and re-layouts  5.77 us

profile of v2, /device:TPU:1, one launch (start us, length us, event | category | flops | bytes accessed | tf_op | source)
XLA Modules:
  0.0 186.2 jit_solution(13390966825579645151)
XLA Ops:
  0.6 179.8 %shard_map.111 = (bf16[128,4096]{1,0:T(8,128)(2,1)}, bf16[128,4096]{1,0:T(8,128)(2,1)}, bf16[128,4096]{1,0:T(8,128)(2,1)}, f32[192,256]{1,0:T(8,128)}) custom-call(s32[16]{0:T(128)} %bucket_ref.1, s32[4]{0:T(128)} %len_ref.1, s32[4]{0:T(128)} %cnt_ref.1, bf16[128,4096]{1,0:T(8,128)(2,1)} %q_in.1, bf16[128,4096]{1,0:T(8,128)(2,1)} %k_in.1, ...), custom_call_target="tpu_custom_call" | custom-call | tf_op jit(solution)/shard_map/pallas_call | solution.py:527
  180.4 0.0 copy-start.1
  180.4 2.4 %copy.16 = bf16[128,4096]{1,0:T(8,128)(2,1)} copy(bf16[128,4096]{1,0:T(8,128)(2,1)} %get-tuple-element.16) | data formatting | bytes 2097152
  182.8 0.0 copy-done.1
  182.8 0.0 copy-start
  182.8 1.0 copy.17
  183.8 0.6 copy-done
  184.4 0.0 copy-start.2
  184.4 1.0 copy.18
  185.4 0.1 copy-done.2
  185.5 0.7 copy.19
Async XLA Ops:
  180.4 2.4 %copy-start.1 = (bf16[128,4096]{1,0:T(8,128)(2,1)S(1)}, bf16[128,4096]{1,0:T(8,128)(2,1)}, u32[]{:S(2)}) copy-start(bf16[128,4096]{1,0:T(8,128)(2,1)} %get-tuple-element.17) | copy-start | bytes 3145732
  182.8 1.6 copy-start
  184.4 1.1 copy-start.2

commit v3 on v2

--- a/solution.py
+++ b/solution.py
@@ -64,6 +64,11 @@
     mate_zh = zh + 1 - 2 * half
     mate = dev(zh_=mate_zh)
     zmate = dev(zl_=1 - zl)
+    free_zh = lax.rem(zh + 3 + 2 * half, 4)
+    free = dev(zh_=free_zh)
+
+    def bt_of(t):
+        return lax.rem(t + 2 * (1 - pair), 4)
 
     def m(v, k):
         return pl.multiple_of(v, k)
@@ -93,8 +98,7 @@
     barrier = pltpu.get_barrier_semaphore()
     peers = [dev(x_=xs_of(d)) for d in (1, 2, 3)]
     peers += [dev(y_=ys_of(d)) for d in (1, 2, 3)]
-    peers += [dev(zh_=lax.rem(zh + d, 4)) for d in (1, 2, 3)]
-    peers += [other, zmate]
+    peers += [mate, free, other, zmate]
     for p in peers:
         pl.semaphore_signal(barrier, inc=1, device_id=p, device_id_type=MESH)
     pl.semaphore_wait(barrier, len(peers))
@@ -116,30 +120,32 @@
 
     mark("first")
 
-    def blocks(src, dst, row, xp):
+    def blocks(src, dst, row, xp, steps):
         out = []
-        for b in range(4):
+        for t in steps:
+            b = bt_of(t)
             out.append((src.at[:, pl.ds(m((b * 4 + xp) * 256, 256), 256)],
-                        dst.at[pl.ds(row, 128), pl.ds(b * 256, 256)]))
+                        dst.at[pl.ds(row, 128), pl.ds(m(b * 256, 256), 256)]))
         return out
 
     arrs = ((q_in, qb, m(row_me, 128)), (k_in, kb, m(x * 128, 128)), (v_in, vb, m(x * 128, 128)))
 
-    def send_x(a):
+    def send_x(a, k, steps):
         src, dst, row = arrs[a]
         for d in (1, 3, 2):
             xp = xs_of(d)
-            for sr, dr in blocks(src, dst, row, xp):
-                send(sr, dr, s_qkv.at[a * 4 + d], r_qkv.at[a, x], dev(x_=xp))
+            for sr, dr in blocks(src, dst, row, xp, steps):
+                send(sr, dr, s_qkv.at[(a * 2 + k) * 4 + d], r_qkv.at[a, k, x], dev(x_=xp))
 
     sends.append(send(
         w_in.at[:, pl.ds(m((1 - core) * 128, 128), 128)], w_got, s_w.at[0], r_wc, other))
     lw = local(w_in.at[:, pl.ds(m(core * 128, 128), 128)], w_own, 0)
-    for a in range(3):
-        send_x(a)
+    send_x(0, 0, (0, 1, 2, 3))
+    send_x(1, 0, (0, 1))
+    send_x(2, 0, (0, 1))
     for a in range(3):
         src, dst, row = arrs[a]
-        for b, (sr, dr) in enumerate(blocks(src, dst, row, x)):
+        for b, (sr, dr) in enumerate(blocks(src, dst, row, x, (0, 1, 2, 3))):
             local(sr, dr, 1 + a * 4 + b)
     local(g_in, gb.at[pl.ds(m(row_me, 128), 128), :], 13)
 
@@ -155,9 +161,8 @@
         return wb.at[pl.ds(m(zh_ * 256 + core * 128, 128), 128), pl.ds(m((y * 2 + zl_) * 384, 128), 384)]
 
     w_blk(zh, zl)[...] = (dot_tn(w_own[...], e_own) + dot_tn(w_got[...], e_oth)).astype(BF)
-    for d in (2, 1, 3):
-        sends.append(send(
-            w_blk(zh, zl), w_blk(zh, zl), s_w.at[d], r_wz.at[zh], dev(zh_=lax.rem(zh + d, 4))))
+    sends.append(send(w_blk(zh, zl), w_blk(zh, zl), s_w.at[1], r_wz.at[zh], mate))
+    sends.append(send(w_blk(zh, zl), w_blk(zh, zl), s_w.at[2], r_wz.at[zh], free))
 
     def g_mate(i):
         sends.append(send(
@@ -178,8 +183,9 @@
                 g_in.at[pl.ds(i * 32, 32), :], g_rows(half, x, i),
                 s_gx.at[i * 2 + j], r_gx.at[0, x, i], p))
     mark("w_z_wait")
-    for d in (1, 3, 2):
-        zs = lax.rem(zh + d, 4)
+    got(w_blk(mate_zh, zl), r_wz.at[mate_zh])
+    sends.append(send(w_blk(mate_zh, zl), w_blk(mate_zh, zl), s_w.at[3], r_wz.at[mate_zh], free))
+    for zs in (free_zh, lax.rem(zh + 2, 4)):
         got(w_blk(zs, zl), r_wz.at[zs])
     for b in range(4):
         sends.append(send(w_blk(b, zl), w_blk(b, zl), s_w.at[4 + b], r_wl.at[b], zmate))
@@ -202,22 +208,22 @@
     for c in loc[1:5]:
         c.wait()
 
-    def bt_of(t):
-        return lax.rem(t + 2 * (1 - pair), 4)
-
     def q_rows(hh, xs):
         return qb.at[pl.ds(m(hh * 512 + xs * 128, 128), 128), :]
 
     for d in (1, 3, 2):
-        got(q_rows(half, xs_of(d)), r_qkv.at[0, xs_of(d)])
+        got(q_rows(half, xs_of(d)), r_qkv.at[0, 0, xs_of(d)])
     own0 = m(half * 512, 512)
     oth0 = m((1 - half) * 512, 512)
 
     def q_blk(r0, t):
         return qb.at[pl.ds(r0, 512), pl.ds(m(bt_of(t) * 256, 256), 256)]
 
-    for t in range(4):
+    def q_send(t):
         sends.append(send(q_blk(own0, t), q_blk(own0, t), s_q2.at[t], r_q2.at[t], mate))
+
+    q_send(0)
+    q_send(1)
 
     def relay(hh, k, i, sem):
         src, to = (xr, left) if i < 2 else (xl, right)
@@ -228,10 +234,14 @@
     for c in loc[5:]:
         c.wait()
     n_loc = len(loc)
-    for a, buf in ((1, kb), (2, vb)):
-        for d in (1, 3, 2):
-            xs = xs_of(d)
-            got(buf.at[pl.ds(m(xs * 128, 128), 128), :], r_qkv.at[a, xs])
+
+    def kv_wait(k):
+        for a, buf in ((1, kb), (2, vb)):
+            for d in (1, 3, 2):
+                xs = xs_of(d)
+                got(buf.at[pl.ds(m(xs * 128, 128), 128), pl.ds(m(bt_of(2 * k) * 256, 256), 512)], r_qkv.at[a, k, xs])
+
+    kv_wait(0)
 
     mark("flip")
     key_pos = lax.broadcasted_iota(jnp.int32, (512, QT), 0) + half * 512
@@ -240,12 +250,13 @@
     def col(h):
         return pl.ds(m(h * 128, 128), 128)
 
-    def flip(h, c):
+    def flip(n, c):
+        h = bt_of(lax.div(n, 2)) * 2 + lax.rem(n, 2)
         kt[col(h), :] = kb[:, col(h)].T
         vt[col(h), :] = vb[:, col(h)].T
         return c
 
-    lax.fori_loop(0, 8, flip, 0)
+    lax.fori_loop(0, 4, flip, 0)
 
     def forward(t, first, r0):
         def body(n, c):
@@ -266,18 +277,34 @@
 
         lax.fori_loop(0, first, body, 0)
 
+    def query(t):
+        mark(f"q_wait_{t}")
+        got(q_blk(oth0, t), r_q2.at[t])
+        mark(f"fwd_{t}")
+        forward(t, 4, oth0)
+
     mark("fwd_own")
-    forward(0, 16, own0)
-
-    for i in (0, 1, 2, 3):
+    forward(0, 8, own0)
+
+    def from_mate(i):
         mark(f"g_mate_{i}")
         got(g_rows(oh, x, i), r_gz.at[i])
         for j, p in enumerate((right, left)):
             sends.append(send(
                 g_rows(oh, x, i), g_rows(oh, x, i), s_gx.at[12 + i * 2 + j], r_gx.at[1, x, i], p))
-    for i in (0, 2, 1, 3):
+
+    def own_relay(i):
         mark(f"g_relay_{i}")
         relay(half, 0, i, 8)
+
+    own_relay(0)
+    own_relay(2)
+    from_mate(0)
+    from_mate(1)
+    own_relay(1)
+    own_relay(3)
+    from_mate(2)
+    from_mate(3)
 
     mark("w_y_wait")
     for d in (1, 3, 2):
@@ -302,6 +329,8 @@
 
         lax.fori_loop(0, 4, body, 0)
 
+    q_send(2)
+    query(0)
     mark("g_own_wait")
     g_rest(half, 0)
     for i in (0, 2):
@@ -317,6 +346,8 @@
     for i in (1, 3):
         mark(f"g_relay2_{i}")
         relay(oh, 1, i, 20)
+    for a in (1, 2):
+        send_x(a, 1, (2, 3))
     mark("grads_own1")
     grads(m(own0 + 256, 256))
 
@@ -373,13 +404,8 @@
         got(gl_got.at[t], r_gl.at[t])
         gz2[t] = (gz[t, zl].astype(F32) + gl_got[t].astype(F32)).astype(BF)
         if t < 2:
-            sends.append(send(gz2.at[t], gz_got.at[half], s_g2.at[t], r_g2.at[half], dev(zh_=bt_of(t))))
-
-    def query(t):
-        mark(f"q_wait_{t}")
-        got(q_blk(oth0, t), r_q2.at[t])
-        mark(f"fwd_{t}")
-        forward(t, 4, oth0)
+            sends.append(send(
+                gz2.at[t], gz_got.at[lax.rem(t + half, 2)], s_g2.at[t], r_g2.at[lax.rem(t + half, 2)], free))
 
     def stats(t):
         mark(f"grads_oth_{t}")
@@ -445,52 +471,63 @@
         lax.fori_loop(0, 4, gw_part, 0)
         sends.append(send(gw_send.at[t], gw_got.at[t], s_gc.at[t], r_gc.at[t], other))
 
-    query(0)
     query(1)
     mark("g_oth_wait")
     g_rest(oh, 1)
     stats(0)
     stats(1)
+    q_send(3)
     merge(0)
     back(0)
     gw(0)
+    mark("kv_wait2")
+    kv_wait(1)
+    mark("flip2")
+    lax.fori_loop(4, 8, flip, 0)
+    mark("fwd_own_2")
+    forward(2, 4, own0)
     query(2)
     stats(2)
     merge(1)
     back(1)
     fold(0)
     gw(1)
+    mark("fwd_own_3")
+    forward(3, 4, own0)
     query(3)
     stats(3)
+    fold(1)
     merge(2)
     gw(2)
     back(2)
-    fold(1)
+    fold(2)
     gather_y(0)
     finish(0)
     merge(3)
     gw(3)
-    fold(2)
+    gather_y(1)
+    fold(3)
     back(3)
-    gather_y(1)
-    fold_l(0)
-    fold(3)
     finish(1)
     gather_y(2)
+    fold_l(0)
     fold_l(1)
+    finish(2)
     gather_y(3)
+    finish(3)
     fold_l(2)
-    finish(2)
     fold_l(3)
+    mark("g_free_wait")
+    got(gz_got.at[0], r_g2.at[0])
+    gz2[3 - half] = (gz2[3 - half].astype(F32) + gz_got[0].astype(F32)).astype(BF)
     sends.append(send(gz2.at[3 - half], gz_got.at[2], s_g2.at[2], r_g2.at[2], mate))
-    finish(3)
 
     mark("gz_wait")
-    for d in range(3):
+    for d in (1, 2):
         got(gz_got.at[d], r_g2.at[d])
     mark("gz_sum")
     v = gz2[2 + half].astype(F32)
-    for d in range(3):
+    for d in (1, 2):
         v = v + gz_got[d].astype(F32)
     fin[...] = v.T
     sends.append(send(
@@ -510,25 +547,36 @@
     mark("send_wait")
     for c in sends:
         c.wait_send()
-    for a in range(3):
-        for d in (1, 2, 3):
-            got(q_rows(half, x), s_qkv.at[a * 4 + d])
+    for d in (1, 2, 3):
+        got(q_rows(half, x), s_qkv.at[d])
+        for a in (1, 2):
+            for k in (0, 1):
+                got(kb.at[pl.ds(0, 128), pl.ds(0, 512)], s_qkv.at[(a * 2 + k) * 4 + d])
     for c in loc[n_loc:]:
         c.wait()
     mark(None)
 
 
+def store(a, b, c, d, ao, bo, co, do, sem):
+    copies = [pltpu.make_async_copy(p, o, sem.at[i]) for i, (p, o) in enumerate(((a, ao), (b, bo), (c, co), (d, do)))]
+    for c in copies:
+        c.start()
+    for c in copies:
+        c.wait()
+
+
 def shards(*args):
     any_ = pl.BlockSpec(memory_space=pl.ANY)
     smem = pl.BlockSpec(memory_space=pltpu.SMEM)
-    tok = jax.ShapeDtypeStruct((128, 4096), BF)
+    vmem = pl.BlockSpec(memory_space=pltpu.VMEM)
+    tok = pltpu.VMEM((128, 4096), BF)
     dma = pltpu.SemaphoreType.DMA
     vm = pltpu.VMEM
-    dq, dk, dv, gw = pl.pallas_call(
+    parts = pl.pallas_call(
         kernel,
-        out_shape=(tok, tok, tok, jax.ShapeDtypeStruct((192, 256), F32)),
+        out_shape=(tok, tok, tok, pltpu.VMEM((192, 256), F32)),
         in_specs=[smem] * 3 + [any_] * 5,
-        out_specs=(any_, any_, any_, pl.BlockSpec(memory_space=pltpu.VMEM)),
+        out_specs=(vmem,) * 4,
         scratch_shapes=[
             vm((1024, 1024), BF), vm((512, 1024), BF), vm((512, 1024), BF),
             vm((1024, 512), BF), vm((1024, 512), BF),
@@ -544,15 +592,24 @@
             vm((4, 4, 128, 768), BF), vm((4, 4, 128, 768), BF),
             vm((4, 2, 128, 384), BF), vm((4, 128, 384), BF), vm((4, 128, 384), BF), vm((3, 128, 384), BF),
             vm((384, 128), F32), vm((192, 128), F32),
-            dma((26,)), dma((12,)), dma((3, 4)), dma((4,)), dma((4,)), dma((4,)), dma((4,)),
+            dma((26,)), dma((24,)), dma((3, 2, 4)), dma((4,)), dma((4,)), dma((4,)), dma((4,)),
             dma((24,)), dma((2, 4, 4)), dma((40,)), dma, dma((4,)), dma((4,)), dma((4, 4)), dma((4, 4)),
             dma((4,)), dma((4,)), dma((4,)), dma((4,)), dma((3, 4, 4)), dma((3, 4, 4)),
             dma((4,)), dma((4,)), dma((4, 4)), dma((4, 4)), dma((4,)), dma((4,)), dma((3,)), dma((3,)), dma((2,)),
         ],
         compiler_params=pltpu.CompilerParams(
-            collective_id=0, has_side_effects=True, vmem_limit_bytes=67043328
+            collective_id=0, has_side_effects=True, vmem_limit_bytes=59768832
         ),
     )(*args[:7], args[7].T)
+    hbm = jax.ShapeDtypeStruct((128, 4096), BF)
+    dq, dk, dv, gw = pl.pallas_call(
+        store,
+        out_shape=(hbm, hbm, hbm, jax.ShapeDtypeStruct((192, 256), F32)),
+        in_specs=[vmem] * 4,
+        out_specs=(any_,) * 4,
+        scratch_shapes=[dma((4,))],
+        compiler_params=pltpu.CompilerParams(vmem_limit_bytes=4194304),
+    )(*parts)
     return dq, dk, dv, gw.T
 
 

time: 186 us -> 168 us (0.903)
  Pallas kernels: 180 us -> 167 us
  local copies, waits for them, and re-layouts: 5.77 us -> 0 us
    pallas_call x1 -> x2, Pallas kernels: 180 us -> 167 us  [the longest x1 165 us: shards(): pl.pallas_call(kernel, out_shape=(tok, tok, tok, pltpu.VMEM((192, 256), F...]
    unnamed x10 -> x0, local copies, waits for them, and re-layouts: 5.77 us -> none
where the time goes in v3:
time: 168 us
  Pallas kernels  167 us (99%)
    pallas_call x1, Pallas kernels, shards(): pl.pallas_call(kernel, out_shape=(tok, tok, tok, pltpu.VMEM((192, 256), F...  165 us

profile of v3, /device:TPU:1, one launch (start us, length us, event | category | flops | bytes accessed | tf_op | source)
XLA Modules:
  0.0 167.5 jit_solution(8663321758796789764)
XLA Ops:
  0.6 165.0 %shard_map.111 = (bf16[128,4096]{1,0:T(8,128)(2,1)S(1)}, bf16[128,4096]{1,0:T(8,128)(2,1)S(1)}, bf16[128,4096]{1,0:T(8,128)(2,1)S(1)}, f32[192,256]{1,0:T(8,128)S(1)}) custom-call(s32[16]{0:T(128)} %bucket_ref.1, s32[4]{0:T(128)} %len_ref.1, s32[4]{0:T(128)} %cnt_ref.1, bf16[128,4096]{1,0:T(8,128)(2,1)} %q_in.1, bf16[128,4096]{1,0:T(8,128)(2,1)} %k_in.1, ...), custom_call_target="tpu_custom_call" | custom-call | tf_op jit(solution)/shard_map/pallas_call | solution.py:575
  165.6 1.8 %shard_map.112 = (bf16[128,4096]{1,0:T(8,128)(2,1)}, bf16[128,4096]{1,0:T(8,128)(2,1)}, bf16[128,4096]{1,0:T(8,128)(2,1)}, f32[192,256]{1,0:T(8,128)}) custom-call(bf16[128,4096]{1,0:T(8,128)(2,1)S(1)} %get-tuple-element.12.a, bf16[128,4096]{1,0:T(8,128)(2,1)S(1)} %get-tuple-element.13.b, bf16[128,4096]{1,0:T(8,128)(2,1)S(1)} %get-tuple-element.14.c, ...), custom_call_target="tpu_custom_call" | custom-call | tf_op jit(solution)/shard_map/pallas_call | solution.py:605
